TPU v7x, 64 devices: a 2x2x8 block of a 4x4x8 slice. The times are simulated.
64 devices in a mesh: rep: 4 (over x, y), dp: 16 (over z, core).
Axes of the slice: x: 2, y: 2, z: 8, core: 2. Of those that a mesh axis runs over, the one named last changes fastest.
The devices are a block of a 4x4x8 slice.
Arguments:
- x: bfloat16 [64, 2048, 512], P(('rep', 'dp')), parts along dimension 0
- dy: bfloat16 [64, 2048, 512], P(('rep', 'dp')), parts along dimension 0
- w_gate: bfloat16 [2, 512, 2560], P(None, 'dp')
- w_up: bfloat16 [2, 512, 2560], P(None, 'dp')
- w_down: bfloat16 [2, 2560, 512], P(None, 'dp')
Outputs:
- output 1: bfloat16 [64, 2048, 512], P(('rep', 'dp')), parts along dimension 0
- output 2: bfloat16 [8, 512, 2560], P('rep', 'dp'), parts along dimension 0
- output 3: bfloat16 [8, 512, 2560], P('rep', 'dp'), parts along dimension 0
- output 4: bfloat16 [8, 2560, 512], P('rep', 'dp'), parts along dimension 0
There are 4 independent parts. A program takes and returns all parts, laid end to end along the dimension named above; an argument that names none is the same for every part.
All inputs are finite; a program needn't handle non-finite values.
Results may differ from a plain program's by a relative error of at most 0.018.
Values are sent between devices in bfloat16 or wider.
A program may use at most 768 MiB of HBM per device.

v0:
```python
import jax
import jax.numpy as jnp
from jax import lax

NAMES = ("w_gate", "w_up", "w_down")


def matmul(a, w):
    return jnp.dot(a, w, preferred_element_type=jnp.float32).astype(jnp.bfloat16)


def normed(h):
    wide = h.astype(jnp.float32)
    scale = lax.rsqrt(jnp.mean(wide**2, -1, keepdims=True) + 1e-6)
    return (wide * scale).astype(jnp.bfloat16)


def layer(h, w):
    a = normed(h)
    gate = jnp.dot(a, w["w_gate"], preferred_element_type=jnp.float32)
    up = jnp.dot(a, w["w_up"], preferred_element_type=jnp.float32)
    return h + matmul((jax.nn.silu(gate) * up).astype(jnp.bfloat16), w["w_down"])


def stack(weights, h):
    for number in range(weights["w_gate"].shape[0]):
        h = layer(h, {name: w[number] for name, w in weights.items()})
    return h


def solution(mesh):
    groups = mesh.shape["rep"]

    def step(x, dy, *weights):
        shape = x.shape
        x, dy = (t.reshape(groups, -1, *t.shape[1:]) for t in (x, dy))

        def of_a_group(x, dy):
            _, back = jax.vjp(stack, dict(zip(NAMES, weights, strict=True)), x)
            by_weights, by_x = back(dy)
            return (by_x, *(by_weights[name] for name in NAMES))

        by_x, *by_weights = jax.vmap(of_a_group)(x, dy)
        return (by_x.reshape(shape), *(t.reshape(-1, *t.shape[2:]) for t in by_weights))

    return step
```

profile of v0, /device:TPU:22, one launch (start us, length us, event | category | flops | bytes accessed | tf_op | source)
XLA Modules:
  0.0 900.3 jit_solution(3319310331275452953)
XLA Ops:
  24.1 25.9 %all-gather.29.cloned.1.call-done = bf16[1,512,2560]{2,1,0:T(8,128)(2,1)} async-done(((bf16[1,32,2560]{2,1,0:T(8,128)(2,1)}), bf16[1,512,2560]{2,1,0:T(8,128)(2,1)}) %all-gather.29.cloned.1.call-update) | async-done | bytes 2621456 | tf_op jit(solution)/vmap(jvp())/squeeze | solution.py:27
  50.0 12.0 %fusion.216 = f32[2048,2560]{1,0:T(8,128)} fusion(bf16[1,512,2560]{2,1,0:T(8,128)(2,1)} %all-gather.29.cloned.1.call-done, bf16[1,2048,512]{2,1,0:T(8,128)(2,1)} %param.13, f32[2048]{0:T(1024)S(1)} %get-tuple-element.267), kind=kOutput, calls=%fused_computation.247 | convolution fusion | flops 5371854848 | bytes 25698304 | tf_op jit(solution)/vmap(jvp())/dot_general | solution.py:20
  62.0 24.7 %all-gather.31.cloned.1.call-done = bf16[1,512,2560]{2,1,0:T(8,128)(2,1)} async-done(((bf16[1,32,2560]{2,1,0:T(8,128)(2,1)}), bf16[1,512,2560]{2,1,0:T(8,128)(2,1)}) %all-gather.31.cloned.1.call-update) | async-done | bytes 2621456 | tf_op jit(solution)/vmap(jvp())/squeeze | solution.py:27
  86.7 18.5 %fusion.168 = (bf16[1,1,2048,2560]{3,2,1,0:T(8,128)(2,1)}, f32[2048,2560]{1,0:T(8,128)}) fusion(f32[2048,2560]{1,0:T(8,128)} %fusion.216, bf16[1,512,2560]{2,1,0:T(8,128)(2,1)} %all-gather.31.cloned.1.call-done, bf16[1,2048,512]{2,1,0:T(8,128)(2,1)} %param.13, f32[2048]{0:T(1024)S(1)} %get-tuple-element.267), kind=kOutput, calls=%fused_computation.195 | convolution fusion | flops 5403312128 | bytes 57155584 | tf_op jit(solution)/vmap(jvp())/dot_general | solution.py:21
  105.3 14.7 %copy.4 = bf16[1,1,2048,2560]{2,3,1,0:T(8,128)(2,1)} copy(bf16[1,1,2048,2560]{3,2,1,0:T(8,128)(2,1)} %get-tuple-element.268) | data formatting | bytes 20971520
  120.0 3.5 all-gather.33.cloned.1.call-done
  123.5 9.3 %fusion.182 = (f32[2048]{0:T(1024)S(1)}, bf16[1,1,2048,512]{2,3,1,0:T(8,128)(2,1)S(1)}) fusion(bf16[1,2560,512]{2,1,0:T(8,128)(2,1)} %all-gather.33.cloned.1.call-done, bf16[1,1,2048,2560]{3,2,1,0:T(8,128)(2,1)} %get-tuple-element.268, bf16[1,2048,512]{1,2,0:T(8,128)(2,1)S(1)} %copy-done.27), kind=kOutput, calls=%fused_computation.225 | convolution fusion | flops 5373949952 | bytes 17309696 | tf_op jit(solution)/vmap(jvp())/dot_general | solution.py:9
  134.6 25.5 %all-gather.37.cloned.1.call-done = bf16[1,2560,512]{2,1,0:T(8,128)(2,1)} async-done(((bf16[1,160,512]{2,1,0:T(8,128)(2,1)}), bf16[1,2560,512]{2,1,0:T(8,128)(2,1)}) %all-gather.37.cloned.1.call-update) | async-done | bytes 2621456 | tf_op jit(solution)/vmap(jvp())/squeeze | solution.py:27
  160.1 10.7 %convolution_convert_fusion.1 = bf16[2048,2560]{1,0:T(8,128)(2,1)} fusion(bf16[1,2560,512]{2,1,0:T(8,128)(2,1)} %all-gather.37.cloned.1.call-done, bf16[1,2048,512]{2,1,0:T(8,128)(2,1)} %param.12), kind=kOutput, calls=%fused_computation.203 | convolution fusion | flops 5373952000 | bytes 15204352 | tf_op jit(solution)/vmap(transpose(jvp()))/dot_general | solution.py:9
  170.8 25.9 %all-gather.39.cloned.1.call-done = bf16[1,512,2560]{2,1,0:T(8,128)(2,1)} async-done(((bf16[1,32,2560]{2,1,0:T(8,128)(2,1)}), bf16[1,512,2560]{2,1,0:T(8,128)(2,1)}) %all-gather.39.cloned.1.call-update) | async-done | bytes 2621456 | tf_op jit(solution)/vmap(jvp())/squeeze | solution.py:27
  196.7 11.7 %fusion.203 = f32[2048,2560]{1,0:T(8,128)} fusion(bf16[1,512,2560]{2,1,0:T(8,128)(2,1)} %all-gather.39.cloned.1.call-done, bf16[1,1,2048,512]{2,3,1,0:T(8,128)(2,1)S(1)} %fusion.183), kind=kOutput, calls=%fused_computation.234 | convolution fusion | flops 5368709120 | bytes 25690112 | tf_op jit(solution)/vmap(jvp())/dot_general | solution.py:21
  208.5 24.9 %all-gather.35.cloned.1.call-done = bf16[1,512,2560]{2,1,0:T(8,128)(2,1)} async-done(((bf16[1,32,2560]{2,1,0:T(8,128)(2,1)}), bf16[1,512,2560]{2,1,0:T(8,128)(2,1)}) %all-gather.35.cloned.1.call-update) | async-done | bytes 2621456 | tf_op jit(solution)/vmap(jvp())/squeeze | solution.py:27
  233.3 28.2 %fusion.153 = (bf16[1,1,2048,2560]{3,2,1,0:T(8,128)(2,1)}, bf16[1,1,2048,2560]{3,2,1,0:T(8,128)(2,1)}, f32[2048,2560]{1,0:T(8,128)}) fusion(f32[2048,2560]{1,0:T(8,128)} %fusion.203, bf16[2048,2560]{1,0:T(8,128)(2,1)} %convolution_convert_fusion.1, bf16[1,512,2560]{2,1,0:T(8,128)(2,1)} %all-gather.35.cloned.1.call-done, ...), kind=kOutput, calls=%fused_computation.175 | convolution fusion | flops 5447352320 | bytes 78118912 | tf_op jit(solution)/vmap(jvp())/dot_general | solution.py:20
  261.5 19.4 %fusion.162 = bf16[1,1,2048,2560]{3,2,1,0:T(8,128)(2,1)} fusion(f32[2048,2560]{1,0:T(8,128)} %fusion.203, f32[2048,2560]{1,0:T(8,128)} %get-tuple-element.272), kind=kLoop, calls=%fused_computation.185 | loop fusion | flops 31457280 | bytes 52428800 | tf_op jit(solution)/vmap(jvp())/convert_element_type | solution.py:22
  280.9 14.6 %copy.2 = bf16[1,1,2048,2560]{2,3,1,0:T(8,128)(2,1)} copy(bf16[1,1,2048,2560]{3,2,1,0:T(8,128)(2,1)} %fusion.162) | data formatting | bytes 20971520
  295.5 71.6 %while.16 = (bf16[1,1,2048,2560]{2,3,1,0:T(8,128)(2,1)}, bf16[1,1,2048,512]{3,2,1,0:T(8,128)(2,1)}, f32[1,160,512]{2,1,0:T(8,128)S(1)}, f32[1,160,512]{2,1,0:T(8...) while((bf16[1,1,2048,2560]{2,3,1,0:T(8,128)(2,1)}, ...), condition=%wide.windowed_dot_general_cond_rs.4.clone, body=%wide.windowed_dot_general_body_rs.4.clone.sunk | while | flops 1347911680 | bytes 87294624 | solution.py:9
  307.9 3.9 collective-permute-done.18
  313.7 3.0 collective-permute-start.17
  326.0 3.9 collective-permute-done.18
  331.8 3.0 collective-permute-start.17
  344.1 3.9 collective-permute-done.18
  350.0 3.0 collective-permute-start.17
  362.2 3.9 collective-permute-done.18
  367.2 9.3 %fusion.188 = bf16[2048,512]{0,1:T(8,128)(2,1)S(1)} fusion(bf16[1,1,2048,2560]{3,2,1,0:T(8,128)(2,1)} %get-tuple-element.628, bf16[1,512,2560]{2,1,0:T(8,128)(2,1)} %all-gather.39.cloned.1.call-done), kind=kOutput, calls=%fused_computation.229 | convolution fusion | flops 5368709120 | bytes 15204352 | tf_op jit(solution)/vmap(transpose(jvp()))/dot_general | solution.py:21
  376.6 8.7 fusion.184
  388.0 4.0 copy.5
  392.0 78.5 %while.17 = (bf16[1,1,2048,2560]{2,3,1,0:T(8,128)(2,1)}, bf16[1,1,2048,512]{3,2,1,0:T(8,128)(2,1)}, f32[1,160,512]{2,1,0:T(8,128)S(1)}, f32[1,160,512]{2,1,0:T(8...) while((bf16[1,1,2048,2560]{2,3,1,0:T(8,128)(2,1)}, ...), condition=%wide.windowed_dot_general_cond_rs.5.clone, body=%wide.windowed_dot_general_body_rs.5.clone.sunk | while | flops 1347911680 | bytes 87294624 | solution.py:9
  392.2 3.0 collective-permute-start.21
  406.2 3.9 collective-permute-done.22
  412.0 3.0 collective-permute-start.21
  426.1 3.9 collective-permute-done.22
  431.9 3.0 collective-permute-start.21
  445.9 3.9 collective-permute-done.22
  451.8 3.0 collective-permute-start.21
  465.8 3.9 collective-permute-done.22
  471.3 88.3 %while.14 = (bf16[1,1,2048,512]{2,3,1,0:T(8,128)(2,1)S(1)}, bf16[1,1,2048,2560]{3,2,1,0:T(8,128)(2,1)}, f32[1,32,2560]{2,1,0:T(8,128)S(1)}, f32[1,32,2560]{2,1,0...) while((bf16[1,1,2048,512]{2,3,1,0:T(8,128)(2,1)S(1)}, ...), condition=%wide.windowed_dot_general_cond_rs.2.clone, body=%wide.windowed_dot_general_body_rs.2.clone.sunk | while | flops 1343717376 | bytes 78905984 | solution.py:21
  476.9 6.0 fusion.331
  499.3 6.0 fusion.331
  521.6 6.0 fusion.331
  543.9 6.0 fusion.331
  559.6 24.4 %fusion.155 = (bf16[1,1,2048,2560]{3,2,1,0:T(8,128)(2,1)S(1)}, bf16[1,1,2048,2560]{3,2,1,0:T(8,128)(2,1)}) fusion(f32[2048,2560]{1,0:T(8,128)} %fusion.216, f32[2048,2560]{1,0:T(8,128)} %get-tuple-element.269, bf16[1,2560,512]{2,1,0:T(8,128)(2,1)} %all-gather.33.cloned.1.call-done, bf16[1,1,2048,512]{2,3,1,0:T(8,128)(2,1)} %fusion.245), kind=kOutput, calls=%fused_computation.177 | convolution fusion | flops 5452595200 | bytes 67633152 | tf_op jit(solution)/vmap(transpose(jvp()))/dot_general | solution.py:9
  584.0 12.9 %fusion.194 = bf16[2048,512]{0,1:T(8,128)(2,1)S(1)} fusion(bf16[1,1,2048,2560]{3,2,1,0:T(8,128)(2,1)} %get-tuple-element.589, bf16[1,512,2560]{2,1,0:T(8,128)(2,1)} %all-gather.31.cloned.1.call-done), kind=kOutput, calls=%fused_computation.231 | convolution fusion | flops 5368709120 | bytes 15204352 | tf_op jit(solution)/vmap(transpose(jvp()))/dot_general | solution.py:21
  597.0 7.5 fusion.181
  604.5 85.1 %while.15 = (bf16[1,1,2048,512]{2,3,1,0:T(8,128)(2,1)}, bf16[1,1,2048,2560]{3,2,1,0:T(8,128)(2,1)}, f32[1,32,2560]{2,1,0:T(8,128)S(1)}, f32[1,32,2560]{2,1,0:T(8...) while((bf16[1,1,2048,512]{2,3,1,0:T(8,128)(2,1)}, ...), condition=%wide.windowed_dot_general_cond_rs.3.clone, body=%wide.windowed_dot_general_body_rs.3.clone.sunk | while | flops 1343717376 | bytes 87294624 | solution.py:21
  610.2 6.2 fusion.339
  631.5 6.2 fusion.339
  652.8 6.2 fusion.339
  674.1 6.2 fusion.339
  690.4 93.8 %while.12 = (bf16[1,1,2048,512]{2,3,1,0:T(8,128)(2,1)S(1)}, bf16[1,1,2048,2560]{3,2,1,0:T(8,128)(2,1)}, f32[1,32,2560]{2,1,0:T(8,128)S(1)}, f32[1,32,2560]{2,1,0...) while((bf16[1,1,2048,512]{2,3,1,0:T(8,128)(2,1)S(1)}, ...), condition=%wide.windowed_dot_general_cond_rs.clone, body=%wide.windowed_dot_general_body_rs.clone.sunk | while | flops 1343717376 | bytes 78905984 | solution.py:20
  697.6 6.0 fusion.315
  721.3 6.0 fusion.315
  744.9 6.0 fusion.315
  768.6 6.0 fusion.315
  784.2 87.6 %while.13 = (bf16[1,1,2048,512]{2,3,1,0:T(8,128)(2,1)}, bf16[1,1,2048,2560]{3,2,1,0:T(8,128)(2,1)}, f32[1,32,2560]{2,1,0:T(8,128)S(1)}, f32[1,32,2560]{2,1,0:T(8...) while((bf16[1,1,2048,512]{2,3,1,0:T(8,128)(2,1)}, ...), condition=%wide.windowed_dot_general_cond_rs.1.clone, body=%wide.windowed_dot_general_body_rs.1.clone.sunk | while | flops 1343717376 | bytes 87294624 | solution.py:20
  785.0 3.0 collective-permute-start.5
  790.6 6.2 fusion.323
  806.9 3.0 collective-permute-start.5
  812.5 6.2 fusion.323
  828.9 3.0 collective-permute-start.5
  834.4 6.2 fusion.323
  850.8 3.0 collective-permute-start.5
  856.3 6.1 fusion.323
  872.0 4.9 fusion.244
  877.0 4.0 copy.6
  (535 shorter events, 331.6 us)
Async XLA Ops:
  7.2 42.8 %all-gather.29.cloned.1.call-start = ((), (), s32[]{:S(2)}) async-start(), calls=%async_computation | async-start | bytes 2785280 | tf_op jit(solution)/vmap(jvp())/squeeze | solution.py:27
  9.2 77.5 %all-gather.31.cloned.1.call-start = ((), (), s32[]{:S(2)}) async-start(), calls=%async_computation.1 | async-start | bytes 2785280 | tf_op jit(solution)/vmap(jvp())/squeeze | solution.py:27
  11.1 112.4 %all-gather.33.cloned.1.call-start = ((), (), s32[]{:S(2)}) async-start(), calls=%async_computation.2 | async-start | bytes 2785280 | tf_op jit(solution)/vmap(jvp())/squeeze | solution.py:27
  13.0 147.1 %all-gather.37.cloned.1.call-start = ((), (), s32[]{:S(2)}) async-start(), calls=%async_computation.4 | async-start | bytes 2785280 | tf_op jit(solution)/vmap(jvp())/squeeze | solution.py:27
  13.7 183.1 %all-gather.39.cloned.1.call-start = ((), (), s32[]{:S(2)}) async-start(), calls=%async_computation.5 | async-start | bytes 2785280 | tf_op jit(solution)/vmap(jvp())/squeeze | solution.py:27
  14.3 219.0 %all-gather.35.cloned.1.call-start = ((), (), s32[]{:S(2)}) async-start(), calls=%async_computation.3 | async-start | bytes 2785280 | tf_op jit(solution)/vmap(jvp())/squeeze | solution.py:27
  295.5 8.3 collective-permute-start.16
  295.8 8.1 collective-permute-start.17
  304.0 7.8 collective-permute-start.18
  313.6 8.4 collective-permute-start.16
  313.7 8.3 collective-permute-start.17
  331.7 8.4 collective-permute-start.16
  331.8 8.3 collective-permute-start.17
  349.8 8.4 collective-permute-start.16
  350.0 8.3 collective-permute-start.17
  367.1 516.0 %collective-permute-start.28 = (f32[1,160,512]{2,1,0:T(8,128)}, f32[1,160,512]{2,1,0:T(8,128)}, u32[]{:S(2)}, u32[]{:S(2)}) collective-permute-start(f32[1,160,512]{2,1,0:T(8,128)} %get-tuple-element.45), channel_id=41, source_target_pairs={{0,1},{1,2},{2,3},{3,4},{4,5},{5,6},{6,7},{7,8},{8,9},{9,10},{10,1... | collective-permute-start | bytes 983048 | tf_op jit(solution)/vmap(transpose(jvp()))/dot_general | solution.py:9
  392.1 8.4 collective-permute-start.20
  392.2 8.3 collective-permute-start.21
  411.9 8.4 collective-permute-start.20
  412.0 8.3 collective-permute-start.21
  431.8 8.4 collective-permute-start.20
  431.9 8.3 collective-permute-start.21
  442.1 7.8 collective-permute-start.22
  451.6 8.4 collective-permute-start.20
  451.8 8.3 collective-permute-start.21
  470.5 413.6 %collective-permute-start.29 = (f32[1,160,512]{2,1,0:T(8,128)}, f32[1,160,512]{2,1,0:T(8,128)}, u32[]{:S(2)}, u32[]{:S(2)}) collective-permute-start(f32[1,160,512]{2,1,0:T(8,128)} %get-tuple-element.47), channel_id=47, source_target_pairs={{0,1},{1,2},{2,3},{3,4},{4,5},{5,6},{6,7},{7,8},{8,9},{9,10},{10,1... | collective-permute-start | bytes 983048 | tf_op jit(solution)/vmap(transpose(jvp()))/dot_general | solution.py:9
  471.3 11.7 %collective-permute-start.8 = (f32[1,32,2560]{2,1,0:T(8,128)S(1)}, f32[1,32,2560]{2,1,0:T(8,128)}, u32[]{:S(2)}, u32[]{:S(2)}) collective-permute-start(f32[1,32,2560]{2,1,0:T(8,128)S(1)} %broadcast_select_fusion.28), channel_id=26, source_target_pairs={{0,1},{1,2},{2,3},{3,4},{4,5},{5,6},{6,7},{7,8},{8,9},{9,10},{10,1... | collective-permute-start | bytes 983048 | tf_op jit(solution)/vmap(transpose(jvp()))/dot_general | solution.py:21
  471.4 11.6 %collective-permute-start.9 = (f32[1,32,2560]{2,1,0:T(8,128)S(1)}, f32[1,32,2560]{2,1,0:T(8,128)S(1)}, u32[]{:S(2)}, u32[]{:S(2)}) collective-permute-start(f32[1,32,2560]{2,1,0:T(8,128)S(1)} %broadcast_select_fusion.29), channel_id=25, source_target_pairs={{0,15},{1,0},{2,1},{3,2},{4,3},{5,4},{6,5},{7,6},{8,7},{9,8},{10,9... | collective-permute-start | bytes 983048 | tf_op jit(solution)/vmap(transpose(jvp()))/dot_general | solution.py:21
  493.6 11.7 %collective-permute-start.8 = (f32[1,32,2560]{2,1,0:T(8,128)S(1)}, f32[1,32,2560]{2,1,0:T(8,128)}, u32[]{:S(2)}, u32[]{:S(2)}) collective-permute-start(f32[1,32,2560]{2,1,0:T(8,128)S(1)} %broadcast_select_fusion.28), channel_id=26, source_target_pairs={{0,1},{1,2},{2,3},{3,4},{4,5},{5,6},{6,7},{7,8},{8,9},{9,10},{10,1... | collective-permute-start | bytes 983048 | tf_op jit(solution)/vmap(transpose(jvp()))/dot_general | solution.py:21
  493.7 11.6 %collective-permute-start.9 = (f32[1,32,2560]{2,1,0:T(8,128)S(1)}, f32[1,32,2560]{2,1,0:T(8,128)S(1)}, u32[]{:S(2)}, u32[]{:S(2)}) collective-permute-start(f32[1,32,2560]{2,1,0:T(8,128)S(1)} %broadcast_select_fusion.29), channel_id=25, source_target_pairs={{0,15},{1,0},{2,1},{3,2},{4,3},{5,4},{6,5},{7,6},{8,7},{9,8},{10,9... | collective-permute-start | bytes 983048 | tf_op jit(solution)/vmap(transpose(jvp()))/dot_general | solution.py:21
  506.4 7.8 collective-permute-start.10
  515.9 11.7 %collective-permute-start.8 = (f32[1,32,2560]{2,1,0:T(8,128)S(1)}, f32[1,32,2560]{2,1,0:T(8,128)}, u32[]{:S(2)}, u32[]{:S(2)}) collective-permute-start(f32[1,32,2560]{2,1,0:T(8,128)S(1)} %broadcast_select_fusion.28), channel_id=26, source_target_pairs={{0,1},{1,2},{2,3},{3,4},{4,5},{5,6},{6,7},{7,8},{8,9},{9,10},{10,1... | collective-permute-start | bytes 983048 | tf_op jit(solution)/vmap(transpose(jvp()))/dot_general | solution.py:21
  516.0 11.6 %collective-permute-start.9 = (f32[1,32,2560]{2,1,0:T(8,128)S(1)}, f32[1,32,2560]{2,1,0:T(8,128)S(1)}, u32[]{:S(2)}, u32[]{:S(2)}) collective-permute-start(f32[1,32,2560]{2,1,0:T(8,128)S(1)} %broadcast_select_fusion.29), channel_id=25, source_target_pairs={{0,15},{1,0},{2,1},{3,2},{4,3},{5,4},{6,5},{7,6},{8,7},{9,8},{10,9... | collective-permute-start | bytes 983048 | tf_op jit(solution)/vmap(transpose(jvp()))/dot_general | solution.py:21
  538.2 11.7 %collective-permute-start.8 = (f32[1,32,2560]{2,1,0:T(8,128)S(1)}, f32[1,32,2560]{2,1,0:T(8,128)}, u32[]{:S(2)}, u32[]{:S(2)}) collective-permute-start(f32[1,32,2560]{2,1,0:T(8,128)S(1)} %broadcast_select_fusion.28), channel_id=26, source_target_pairs={{0,1},{1,2},{2,3},{3,4},{4,5},{5,6},{6,7},{7,8},{8,9},{9,10},{10,1... | collective-permute-start | bytes 983048 | tf_op jit(solution)/vmap(transpose(jvp()))/dot_general | solution.py:21
  538.4 11.6 %collective-permute-start.9 = (f32[1,32,2560]{2,1,0:T(8,128)S(1)}, f32[1,32,2560]{2,1,0:T(8,128)S(1)}, u32[]{:S(2)}, u32[]{:S(2)}) collective-permute-start(f32[1,32,2560]{2,1,0:T(8,128)S(1)} %broadcast_select_fusion.29), channel_id=25, source_target_pairs={{0,15},{1,0},{2,1},{3,2},{4,3},{5,4},{6,5},{7,6},{8,7},{9,8},{10,9... | collective-permute-start | bytes 983048 | tf_op jit(solution)/vmap(transpose(jvp()))/dot_general | solution.py:21
  551.0 7.8 collective-permute-start.10
  559.6 321.4 %collective-permute-start.26 = (f32[1,32,2560]{2,1,0:T(8,128)}, f32[1,32,2560]{2,1,0:T(8,128)}, u32[]{:S(2)}, u32[]{:S(2)}) collective-permute-start(f32[1,32,2560]{2,1,0:T(8,128)} %get-tuple-element.41), channel_id=29, source_target_pairs={{0,1},{1,2},{2,3},{3,4},{4,5},{5,6},{6,7},{7,8},{8,9},{9,10},{10,1... | collective-permute-start | bytes 983048 | tf_op jit(solution)/vmap(transpose(jvp()))/dot_general | solution.py:21
  604.6 11.8 %collective-permute-start.12 = (f32[1,32,2560]{2,1,0:T(8,128)S(1)}, f32[1,32,2560]{2,1,0:T(8,128)}, u32[]{:S(2)}, u32[]{:S(2)}) collective-permute-start(f32[1,32,2560]{2,1,0:T(8,128)S(1)} %broadcast_select_fusion.30), channel_id=32, source_target_pairs={{0,1},{1,2},{2,3},{3,4},{4,5},{5,6},{6,7},{7,8},{8,9},{9,10},{10,1... | collective-permute-start | bytes 983048 | tf_op jit(solution)/vmap(transpose(jvp()))/dot_general | solution.py:21
  604.7 11.7 %collective-permute-start.13 = (f32[1,32,2560]{2,1,0:T(8,128)S(1)}, f32[1,32,2560]{2,1,0:T(8,128)S(1)}, u32[]{:S(2)}, u32[]{:S(2)}) collective-permute-start(f32[1,32,2560]{2,1,0:T(8,128)S(1)} %broadcast_select_fusion.31), channel_id=31, source_target_pairs={{0,15},{1,0},{2,1},{3,2},{4,3},{5,4},{6,5},{7,6},{8,7},{9,8},{10,9... | collective-permute-start | bytes 983048 | tf_op jit(solution)/vmap(transpose(jvp()))/dot_general | solution.py:21
  618.0 7.8 collective-permute-start.14
  625.8 11.8 %collective-permute-start.12 = (f32[1,32,2560]{2,1,0:T(8,128)S(1)}, f32[1,32,2560]{2,1,0:T(8,128)}, u32[]{:S(2)}, u32[]{:S(2)}) collective-permute-start(f32[1,32,2560]{2,1,0:T(8,128)S(1)} %broadcast_select_fusion.30), channel_id=32, source_target_pairs={{0,1},{1,2},{2,3},{3,4},{4,5},{5,6},{6,7},{7,8},{8,9},{9,10},{10,1... | collective-permute-start | bytes 983048 | tf_op jit(solution)/vmap(transpose(jvp()))/dot_general | solution.py:21
  626.0 11.7 %collective-permute-start.13 = (f32[1,32,2560]{2,1,0:T(8,128)S(1)}, f32[1,32,2560]{2,1,0:T(8,128)S(1)}, u32[]{:S(2)}, u32[]{:S(2)}) collective-permute-start(f32[1,32,2560]{2,1,0:T(8,128)S(1)} %broadcast_select_fusion.31), channel_id=31, source_target_pairs={{0,15},{1,0},{2,1},{3,2},{4,3},{5,4},{6,5},{7,6},{8,7},{9,8},{10,9... | collective-permute-start | bytes 983048 | tf_op jit(solution)/vmap(transpose(jvp()))/dot_general | solution.py:21
  647.1 11.8 %collective-permute-start.12 = (f32[1,32,2560]{2,1,0:T(8,128)S(1)}, f32[1,32,2560]{2,1,0:T(8,128)}, u32[]{:S(2)}, u32[]{:S(2)}) collective-permute-start(f32[1,32,2560]{2,1,0:T(8,128)S(1)} %broadcast_select_fusion.30), channel_id=32, source_target_pairs={{0,1},{1,2},{2,3},{3,4},{4,5},{5,6},{6,7},{7,8},{8,9},{9,10},{10,1... | collective-permute-start | bytes 983048 | tf_op jit(solution)/vmap(transpose(jvp()))/dot_general | solution.py:21
  647.2 11.7 %collective-permute-start.13 = (f32[1,32,2560]{2,1,0:T(8,128)S(1)}, f32[1,32,2560]{2,1,0:T(8,128)S(1)}, u32[]{:S(2)}, u32[]{:S(2)}) collective-permute-start(f32[1,32,2560]{2,1,0:T(8,128)S(1)} %broadcast_select_fusion.31), channel_id=31, source_target_pairs={{0,15},{1,0},{2,1},{3,2},{4,3},{5,4},{6,5},{7,6},{8,7},{9,8},{10,9... | collective-permute-start | bytes 983048 | tf_op jit(solution)/vmap(transpose(jvp()))/dot_general | solution.py:21
  668.4 11.8 %collective-permute-start.12 = (f32[1,32,2560]{2,1,0:T(8,128)S(1)}, f32[1,32,2560]{2,1,0:T(8,128)}, u32[]{:S(2)}, u32[]{:S(2)}) collective-permute-start(f32[1,32,2560]{2,1,0:T(8,128)S(1)} %broadcast_select_fusion.30), channel_id=32, source_target_pairs={{0,1},{1,2},{2,3},{3,4},{4,5},{5,6},{6,7},{7,8},{8,9},{9,10},{10,1... | collective-permute-start | bytes 983048 | tf_op jit(solution)/vmap(transpose(jvp()))/dot_general | solution.py:21
  668.5 11.7 %collective-permute-start.13 = (f32[1,32,2560]{2,1,0:T(8,128)S(1)}, f32[1,32,2560]{2,1,0:T(8,128)S(1)}, u32[]{:S(2)}, u32[]{:S(2)}) collective-permute-start(f32[1,32,2560]{2,1,0:T(8,128)S(1)} %broadcast_select_fusion.31), channel_id=31, source_target_pairs={{0,15},{1,0},{2,1},{3,2},{4,3},{5,4},{6,5},{7,6},{8,7},{9,8},{10,9... | collective-permute-start | bytes 983048 | tf_op jit(solution)/vmap(transpose(jvp()))/dot_general | solution.py:21
  691.4 12.3 %collective-permute-start = (f32[1,32,2560]{2,1,0:T(8,128)}, f32[1,32,2560]{2,1,0:T(8,128)}, u32[]{:S(2)}, u32[]{:S(2)}) collective-permute-start(f32[1,32,2560]{2,1,0:T(8,128)} %broadcast_select_fusion.24), channel_id=14, source_target_pairs={{0,1},{1,2},{2,3},{3,4},{4,5},{5,6},{6,7},{7,8},{8,9},{9,10},{10,1... | collective-permute-start | bytes 983048 | tf_op jit(solution)/vmap(transpose(jvp()))/dot_general | solution.py:20
  692.1 11.5 %collective-permute-start.1 = (f32[1,32,2560]{2,1,0:T(8,128)}, f32[1,32,2560]{2,1,0:T(8,128)S(1)}, u32[]{:S(2)}, u32[]{:S(2)}) collective-permute-start(f32[1,32,2560]{2,1,0:T(8,128)} %broadcast_select_fusion.25), channel_id=13, source_target_pairs={{0,15},{1,0},{2,1},{3,2},{4,3},{5,4},{6,5},{7,6},{8,7},{9,8},{10,9... | collective-permute-start | bytes 983048 | tf_op jit(solution)/vmap(transpose(jvp()))/dot_general | solution.py:20
  715.0 12.3 %collective-permute-start = (f32[1,32,2560]{2,1,0:T(8,128)}, f32[1,32,2560]{2,1,0:T(8,128)}, u32[]{:S(2)}, u32[]{:S(2)}) collective-permute-start(f32[1,32,2560]{2,1,0:T(8,128)} %broadcast_select_fusion.24), channel_id=14, source_target_pairs={{0,1},{1,2},{2,3},{3,4},{4,5},{5,6},{6,7},{7,8},{8,9},{9,10},{10,1... | collective-permute-start | bytes 983048 | tf_op jit(solution)/vmap(transpose(jvp()))/dot_general | solution.py:20
  715.8 11.5 %collective-permute-start.1 = (f32[1,32,2560]{2,1,0:T(8,128)}, f32[1,32,2560]{2,1,0:T(8,128)S(1)}, u32[]{:S(2)}, u32[]{:S(2)}) collective-permute-start(f32[1,32,2560]{2,1,0:T(8,128)} %broadcast_select_fusion.25), channel_id=13, source_target_pairs={{0,15},{1,0},{2,1},{3,2},{4,3},{5,4},{6,5},{7,6},{8,7},{9,8},{10,9... | collective-permute-start | bytes 983048 | tf_op jit(solution)/vmap(transpose(jvp()))/dot_general | solution.py:20
  738.7 12.3 %collective-permute-start = (f32[1,32,2560]{2,1,0:T(8,128)}, f32[1,32,2560]{2,1,0:T(8,128)}, u32[]{:S(2)}, u32[]{:S(2)}) collective-permute-start(f32[1,32,2560]{2,1,0:T(8,128)} %broadcast_select_fusion.24), channel_id=14, source_target_pairs={{0,1},{1,2},{2,3},{3,4},{4,5},{5,6},{6,7},{7,8},{8,9},{9,10},{10,1... | collective-permute-start | bytes 983048 | tf_op jit(solution)/vmap(transpose(jvp()))/dot_general | solution.py:20
  739.4 11.5 %collective-permute-start.1 = (f32[1,32,2560]{2,1,0:T(8,128)}, f32[1,32,2560]{2,1,0:T(8,128)S(1)}, u32[]{:S(2)}, u32[]{:S(2)}) collective-permute-start(f32[1,32,2560]{2,1,0:T(8,128)} %broadcast_select_fusion.25), channel_id=13, source_target_pairs={{0,15},{1,0},{2,1},{3,2},{4,3},{5,4},{6,5},{7,6},{8,7},{9,8},{10,9... | collective-permute-start | bytes 983048 | tf_op jit(solution)/vmap(transpose(jvp()))/dot_general | solution.py:20
  762.3 12.3 %collective-permute-start = (f32[1,32,2560]{2,1,0:T(8,128)}, f32[1,32,2560]{2,1,0:T(8,128)}, u32[]{:S(2)}, u32[]{:S(2)}) collective-permute-start(f32[1,32,2560]{2,1,0:T(8,128)} %broadcast_select_fusion.24), channel_id=14, source_target_pairs={{0,1},{1,2},{2,3},{3,4},{4,5},{5,6},{6,7},{7,8},{8,9},{9,10},{10,1... | collective-permute-start | bytes 983048 | tf_op jit(solution)/vmap(transpose(jvp()))/dot_general | solution.py:20
  763.1 11.5 %collective-permute-start.1 = (f32[1,32,2560]{2,1,0:T(8,128)}, f32[1,32,2560]{2,1,0:T(8,128)S(1)}, u32[]{:S(2)}, u32[]{:S(2)}) collective-permute-start(f32[1,32,2560]{2,1,0:T(8,128)} %broadcast_select_fusion.25), channel_id=13, source_target_pairs={{0,15},{1,0},{2,1},{3,2},{4,3},{5,4},{6,5},{7,6},{8,7},{9,8},{10,9... | collective-permute-start | bytes 983048 | tf_op jit(solution)/vmap(transpose(jvp()))/dot_general | solution.py:20
  785.0 11.7 %collective-permute-start.4 = (f32[1,32,2560]{2,1,0:T(8,128)}, f32[1,32,2560]{2,1,0:T(8,128)}, u32[]{:S(2)}, u32[]{:S(2)}) collective-permute-start(f32[1,32,2560]{2,1,0:T(8,128)} %broadcast_select_fusion.26), channel_id=20, source_target_pairs={{0,1},{1,2},{2,3},{3,4},{4,5},{5,6},{6,7},{7,8},{8,9},{9,10},{10,1... | collective-permute-start | bytes 983048 | tf_op jit(solution)/vmap(transpose(jvp()))/dot_general | solution.py:20
  785.0 11.7 %collective-permute-start.5 = (f32[1,32,2560]{2,1,0:T(8,128)S(1)}, f32[1,32,2560]{2,1,0:T(8,128)S(1)}, u32[]{:S(2)}, u32[]{:S(2)}) collective-permute-start(f32[1,32,2560]{2,1,0:T(8,128)S(1)} %broadcast_select_fusion.27), channel_id=19, source_target_pairs={{0,15},{1,0},{2,1},{3,2},{4,3},{5,4},{6,5},{7,6},{8,7},{9,8},{10,9... | collective-permute-start | bytes 983048 | tf_op jit(solution)/vmap(transpose(jvp()))/dot_general | solution.py:20
  806.9 11.7 %collective-permute-start.4 = (f32[1,32,2560]{2,1,0:T(8,128)}, f32[1,32,2560]{2,1,0:T(8,128)}, u32[]{:S(2)}, u32[]{:S(2)}) collective-permute-start(f32[1,32,2560]{2,1,0:T(8,128)} %broadcast_select_fusion.26), channel_id=20, source_target_pairs={{0,1},{1,2},{2,3},{3,4},{4,5},{5,6},{6,7},{7,8},{8,9},{9,10},{10,1... | collective-permute-start | bytes 983048 | tf_op jit(solution)/vmap(transpose(jvp()))/dot_general | solution.py:20
  806.9 11.7 %collective-permute-start.5 = (f32[1,32,2560]{2,1,0:T(8,128)S(1)}, f32[1,32,2560]{2,1,0:T(8,128)S(1)}, u32[]{:S(2)}, u32[]{:S(2)}) collective-permute-start(f32[1,32,2560]{2,1,0:T(8,128)S(1)} %broadcast_select_fusion.27), channel_id=19, source_target_pairs={{0,15},{1,0},{2,1},{3,2},{4,3},{5,4},{6,5},{7,6},{8,7},{9,8},{10,9... | collective-permute-start | bytes 983048 | tf_op jit(solution)/vmap(transpose(jvp()))/dot_general | solution.py:20
  828.8 11.7 %collective-permute-start.4 = (f32[1,32,2560]{2,1,0:T(8,128)}, f32[1,32,2560]{2,1,0:T(8,128)}, u32[]{:S(2)}, u32[]{:S(2)}) collective-permute-start(f32[1,32,2560]{2,1,0:T(8,128)} %broadcast_select_fusion.26), channel_id=20, source_target_pairs={{0,1},{1,2},{2,3},{3,4},{4,5},{5,6},{6,7},{7,8},{8,9},{9,10},{10,1... | collective-permute-start | bytes 983048 | tf_op jit(solution)/vmap(transpose(jvp()))/dot_general | solution.py:20
  828.9 11.7 %collective-permute-start.5 = (f32[1,32,2560]{2,1,0:T(8,128)S(1)}, f32[1,32,2560]{2,1,0:T(8,128)S(1)}, u32[]{:S(2)}, u32[]{:S(2)}) collective-permute-start(f32[1,32,2560]{2,1,0:T(8,128)S(1)} %broadcast_select_fusion.27), channel_id=19, source_target_pairs={{0,15},{1,0},{2,1},{3,2},{4,3},{5,4},{6,5},{7,6},{8,7},{9,8},{10,9... | collective-permute-start | bytes 983048 | tf_op jit(solution)/vmap(transpose(jvp()))/dot_general | solution.py:20
  850.7 11.7 %collective-permute-start.4 = (f32[1,32,2560]{2,1,0:T(8,128)}, f32[1,32,2560]{2,1,0:T(8,128)}, u32[]{:S(2)}, u32[]{:S(2)}) collective-permute-start(f32[1,32,2560]{2,1,0:T(8,128)} %broadcast_select_fusion.26), channel_id=20, source_target_pairs={{0,1},{1,2},{2,3},{3,4},{4,5},{5,6},{6,7},{7,8},{8,9},{9,10},{10,1... | collective-permute-start | bytes 983048 | tf_op jit(solution)/vmap(transpose(jvp()))/dot_general | solution.py:20
  850.8 11.7 %collective-permute-start.5 = (f32[1,32,2560]{2,1,0:T(8,128)S(1)}, f32[1,32,2560]{2,1,0:T(8,128)S(1)}, u32[]{:S(2)}, u32[]{:S(2)}) collective-permute-start(f32[1,32,2560]{2,1,0:T(8,128)S(1)} %broadcast_select_fusion.27), channel_id=19, source_target_pairs={{0,15},{1,0},{2,1},{3,2},{4,3},{5,4},{6,5},{7,6},{8,7},{9,8},{10,9... | collective-permute-start | bytes 983048 | tf_op jit(solution)/vmap(transpose(jvp()))/dot_general | solution.py:20
  871.9 10.2 %collective-permute-start.27 = (f32[1,32,2560]{2,1,0:T(8,128)}, f32[1,32,2560]{2,1,0:T(8,128)}, u32[]{:S(2)}, u32[]{:S(2)}) collective-permute-start(f32[1,32,2560]{2,1,0:T(8,128)} %copy-done.34), channel_id=35, source_target_pairs={{0,1},{1,2},{2,3},{3,4},{4,5},{5,6},{6,7},{7,8},{8,9},{9,10},{10,1... | collective-permute-start | bytes 983048 | tf_op jit(solution)/vmap(transpose(jvp()))/dot_general | solution.py:21
  881.0 11.2 %collective-permute-start.25 = (f32[1,32,2560]{2,1,0:T(8,128)S(1)}, f32[1,32,2560]{2,1,0:T(8,128)S(1)}, u32[]{:S(2)}, u32[]{:S(2)}) collective-permute-start(f32[1,32,2560]{2,1,0:T(8,128)S(1)} %get-tuple-element.39), channel_id=23, source_target_pairs={{0,1},{1,2},{2,3},{3,4},{4,5},{5,6},{6,7},{7,8},{8,9},{9,10},{10,1... | collective-permute-start | bytes 983048 | tf_op jit(solution)/vmap(transpose(jvp()))/dot_general | solution.py:20
  (119 other events, 1510.5 us)
Sparse Core Ops, SparseCore 0:
  9.6 40.3 all-gather.28
  51.6 35.0 all-gather.30
  88.4 35.0 all-gather.32
  125.0 35.0 all-gather.36
  161.6 35.0 all-gather.38
  198.2 35.0 all-gather.34
where the time goes:
time: 911 us; the launch traced here: 900 us
  matrix products  311 us (34%)
  waiting for transfers between devices  215 us (24%)
  starting transfers between devices  145 us (16%)
  other arithmetic  98.5 us (11%)
  local copies, waits for them, and re-layouts  68.4 us (8%)
  loops' own time  46.7 us (5%)
  between operations  15.1 us (2%)
    squeeze x6, waiting for transfers between devices, stack(): h = layer(h, {name: w[number] for name, w in weights.items()})  130 us
    dot_general x20, matrix products, layer(): gate = jnp.dot(a, w['w_gate'], preferred_element_type=jnp.float32)  120 us
    dot_general x20, matrix products, layer(): up = jnp.dot(a, w['w_up'], preferred_element_type=jnp.float32)  116 us
    dot_general x19, matrix products, matmul(): jnp.dot(a, w, preferred_element_type=jnp.float32).astype(jnp.bfloat16)  74.8 us
    dot_general x34, starting transfers between devices, layer(): up = jnp.dot(a, w['w_up'], preferred_element_type=jnp.float32)  48.6 us
    dot_general x34, starting transfers between devices, matmul(): jnp.dot(a, w, preferred_element_type=jnp.float32).astype(jnp.bfloat16)  48.6 us
    unnamed x77, local copies, waits for them, and re-layouts  48.1 us
    dot_general x34, starting transfers between devices, layer(): gate = jnp.dot(a, w['w_gate'], preferred_element_type=jnp.float32)  47.9 us
  transfers between devices with their start and end apart: 108, of which 32 were waited for; matrix products, arithmetic and copies ran while one was open for 45% of the time, Pallas kernels for 0%

commit v1 on v0

v1 whole, which is shorter than its diff:
```python
import functools
import math

import jax
import jax.numpy as jnp
from jax import lax
from jax.experimental import pallas as pl
from jax.experimental.pallas import tpu as pltpu
from jax.sharding import PartitionSpec as P

MESH = pl.DeviceIdType.MESH
F32, BF16 = jnp.float32, jnp.bfloat16
TILE = 512
DELAY = 2


def dot(a, b):
    return jnp.dot(a, b, preferred_element_type=F32)


def dot_t(a, b):
    return lax.dot_general(a, b, (((1,), (1,)), ((), ())), preferred_element_type=F32)


def rms_scale(wide):
    return lax.rsqrt(jnp.mean(wide * wide, -1, keepdims=True) + 1e-6)


def kernel(cfg, x_hbm, dy_hbm, wg_hbm, wu_hbm, wd_hbm, dx_hbm, g_hbm, u_hbm, d_hbm,
           WGU, WD, H, A, AT, DY, DYT, DGU, PJ, DWD, TK, SIB, SEND, RECV, OG, OU, OD,
           load_sem, ag_send, ag_recv, xy_send, xy_recv, sib_send, sib_recv,
           tk_send, tk_recv, msg_send, msg_recv, out_sem):
    n, side, xy, tokens, d, ff = cfg
    fb = d // 2
    half = ff // 2
    per_half = half // fb
    blocks = ff // fb
    rb = d // (2 * n)
    db = ff // (2 * n)
    kw = db // rb
    layer_slots = blocks + kw
    tickets = 2 * layer_slots
    far = n // 2
    ring = DELAY * far + 2
    tile = min(TILE, tokens // 4)
    tiles = tokens // tile
    tile_c = min(512, tokens // 4)
    tiles_c = tokens // tile_c

    me = lax.axis_index("dp")
    z, c = me // 2, me % 2
    rep = lax.axis_index("rep")
    right = {"dp": lax.rem(z + 1, n) * 2 + c}
    left = {"dp": lax.rem(z + n - 1, n) * 2 + c}
    partner = {"dp": z * 2 + 1 - c}
    gx, gy = rep // side, rep % side
    x_next = {"rep": (gx + 1 - 2 * (gx % 2)) * side + gy}
    y_next = {"rep": gx * side + gy + 1 - 2 * (gy % 2)}
    parity = (gx + gy) % 2

    def remote(src, dst, ss, rs, to):
        return pltpu.make_async_remote_copy(src_ref=src, dst_ref=dst, send_sem=ss, recv_sem=rs, device_id=to, device_id_type=MESH)

    def at(k):
        return lax.rem(z + k + 2 * n, n)

    AG = [(0, "gu", 0), (0, "gu", 1), (0, "wd", 0), (1, "wd", 0), (1, "gu", 0), (1, "gu", 1)]
    own_g = pl.ds(pl.multiple_of(me * rb, rb), rb)
    own_d = pl.ds(pl.multiple_of(me * db, rb), db)
    loads = []
    for t, (l, kind, h) in enumerate(AG):
        if kind == "gu":
            for m, w in enumerate((wg_hbm, wu_hbm)):
                loads.append((t, pltpu.make_async_copy(w.at[l, :, pl.ds(h * half, half)],
                                                       WGU.at[l, own_g, pl.ds((2 * h + m) * half, half)], load_sem.at[2 * t + m])))
        else:
            loads.append((t, pltpu.make_async_copy(wd_hbm.at[l], WD.at[l, own_d, :], load_sem.at[2 * t])))
    for _, copy in loads:
        copy.start()
    load_x = pltpu.make_async_copy(x_hbm.at[0], H, load_sem.at[2 * len(AG)])
    load_dy = pltpu.make_async_copy(dy_hbm.at[0], DY, load_sem.at[2 * len(AG) + 1])
    load_x.start()
    load_dy.start()

    barrier = pltpu.get_barrier_semaphore()
    friends = [left, right, partner] + ([x_next, y_next] if xy else [])
    for friend in friends:
        pl.semaphore_signal(barrier, inc=1, device_id=friend, device_id_type=MESH)
    pl.semaphore_wait(barrier, len(friends))

    share = 2 if xy else 1

    def piece(t, chip, part, cols):
        l, kind, h = AG[t]
        ref, rows, width, base = (WGU, rb, 2 * half, h * 2 * half) if kind == "gu" else (WD, db, d, 0)
        start = (2 * chip + c) * rows
        count = rows
        if part is not None:
            count = rows // 2
            start = start + part * count
        unit = math.gcd(rows, count)
        cw = width if cols is None else width // 2
        return ref.at[l, pl.ds(pl.multiple_of(start, math.gcd(unit, 16)), count), pl.ds(base + (cols or 0) * cw, cw)]

    def many(t, pieces, part, cols):
        l, kind, h = AG[t]
        ref, rows, width = (WGU, rb, 2 * half) if kind == "gu" else (WD, db, d)
        return ref.at[l, pl.ds(0, pieces * (rows // 2 if part else rows)), pl.ds(0, width // 2 if cols else width)]

    mine = parity if xy else None

    def hop(t, k, way):
        p = piece(t, at(-k if way == 0 else k), mine, way if k + 1 == n // 2 else None)
        return remote(p, p, ag_send.at[t, k, way], ag_recv.at[t, k, way], (right, left)[way])

    def arrive(t, k, way):
        p = piece(t, at(-(k + 1) if way == 0 else k + 1), mine, way if k + 1 == n // 2 else None)
        return remote(p, p, ag_send.at[t, k, way], ag_recv.at[t, k, way], (right, left)[way])

    def to_groups(t, chip):
        for m, friend in enumerate((x_next, y_next)):
            p = piece(t, chip, mine, m)
            remote(p, p, xy_send.at[t, m], xy_recv.at[t, m], friend).start()

    def group_wait(t, m):
        p = many(t, n - 1, True, True)
        return remote(p, p, xy_send.at[t, m], xy_recv.at[t, m], (x_next, y_next)[m])

    def partner_wait(t):
        p = many(t, n, None, None)
        return remote(p, p, sib_send.at[t], sib_recv.at[t], partner)

    def to_partner(t, chip, part):
        p = piece(t, chip, part, None)
        remote(p, p, sib_send.at[t], sib_recv.at[t], partner).start()

    def ag_step(t, k):
        if k == 0:
            for owner, copy in loads:
                if owner == t:
                    copy.wait()
            for way in (0, 1):
                hop(t, 0, way).start()
            to_partner(t, z, None)
        elif k <= n // 2:
            for way in (0, 1):
                arrive(t, k - 1, way).wait_recv()
                if k < n // 2:
                    hop(t, k, way).start()
            for chip in [at(-k), at(k)] if k < n // 2 else [at(k)]:
                if xy:
                    to_groups(t, chip)
                to_partner(t, chip, mine)
        elif k == n // 2 + 1 and xy:
            for m in (0, 1):
                group_wait(t, m).wait_recv()
            for b in range(1, n):
                to_partner(t, at(b), 1 - parity)

    last = n // 2 + 1
    rounds = len(AG) + last

    def ag_round(r):
        for t in range(len(AG)):
            if 0 <= r - t <= last:
                ag_step(t, r - t)

    def ready_round(t):
        return t + last

    for r in range(2):
        ag_round(r)
    load_x.wait()

    def turned(ref, ts, a):
        unit = (lax.broadcasted_iota(jnp.int32, (fb, fb), 0) == lax.broadcasted_iota(jnp.int32, (fb, fb), 1)).astype(F32).astype(BF16)
        for m in range(d // fb):
            ref[m * fb:(m + 1) * fb, ts] = dot_t(unit, a[:, m * fb:(m + 1) * fb]).astype(BF16)

    def normed_into(with_t):
        for i in range(tiles):
            ts = pl.ds(i * tile, tile)
            wide = H[ts, :].astype(F32)
            a = (wide * rms_scale(wide)).astype(BF16)
            A[ts, :] = a
            if with_t:
                turned(AT, ts, a)

    def transpose_dy():
        for i in range(tiles):
            ts = pl.ds(i * tile, tile)
            turned(DYT, ts, DY[ts, :])

    normed_into(False)
    load_dy.wait()
    transpose_dy()

    def columns(j):
        g = (j // per_half) * 2 * half + (j % per_half) * fb
        return pl.ds(pl.multiple_of(g, fb), fb), pl.ds(pl.multiple_of(g + half, fb), fb)

    def forward_block(j, _):
        gc, uc = columns(j)
        wg, wu = WGU[0, :, gc], WGU[0, :, uc]
        for i in range(tiles):
            ts = pl.ds(i * tile, tile)
            a = A[ts, :]
            g, u = dot(a, wg), dot(a, wu)
            s = 0.5 * jnp.tanh(0.5 * g) + 0.5
            DGU[ts, pl.ds(pl.multiple_of(j * fb, fb), fb)] = (g * s * u).astype(BF16)
        return 0

    for r in range(2, ready_round(0) + 1):
        ag_round(r)
    partner_wait(0).wait_recv()
    cut = (per_half + 1) // 2
    lax.fori_loop(0, cut, forward_block, 0)
    ag_round(ready_round(1))
    lax.fori_loop(cut, per_half, forward_block, 0)
    partner_wait(1).wait_recv()
    lax.fori_loop(per_half, per_half + cut, forward_block, 0)
    ag_round(ready_round(2))
    lax.fori_loop(per_half + cut, blocks, forward_block, 0)
    ag_round(ready_round(3))
    partner_wait(2).wait_recv()
    for i in range(tiles):
        ts = pl.ds(i * tile, tile)
        y = dot(DGU[ts, pl.ds(0, ff)], WD[0]).astype(BF16)
        H[ts, :] = H[ts, :] + y
        if i == 1:
            ag_round(ready_round(4))
    normed_into(True)
    for t in (3, 4):
        partner_wait(t).wait_recv()

    def slot_of(u):
        return lax.rem(u + 4 * ring, ring)

    def exchange(u):
        par = lax.rem(u, 2)
        return remote(TK.at[ring + par], SIB.at[slot_of(u)], tk_send.at[par], tk_recv.at[par], partner)

    def message(tau, way, lo):
        box = lax.rem(tau + 2 * DELAY, 2 * DELAY)
        return remote(SEND.at[way, box, pl.ds(lo, n - 1 - lo)], RECV.at[way, box, pl.ds(lo, n - 1 - lo)],
                      msg_send.at[way, box], msg_recv.at[way, box], (right, left)[way])

    def stage_of(tau):
        return max(0, -(-(tau - tickets) // DELAY)) if isinstance(tau, int) else 0

    def lowest(tau):
        return max(0, 2 * stage_of(tau) - 1)

    def ticket_row(u, q):
        keep, give = slot_of(u), ring + lax.rem(u + 2, 2)
        return keep + (give - keep) * ((q + c) % 2)

    def own_term(u, chip, part):
        cols = pl.ds(part * fb, fb)
        sl = slot_of(u)
        return TK[sl, chip, :, cols].astype(F32) + SIB[sl, chip, :, cols].astype(F32)

    def when(cond, f):
        if isinstance(cond, bool):
            if cond:
                f()
        else:
            pl.when(cond)(f)

    def spot(stage, way, part):
        return 0 if stage == 0 else 2 * stage - 1 + (part != way)

    def reduce_step(tau):
        static = isinstance(tau, int)
        box, came = lax.rem(tau + 2 * DELAY, 2 * DELAY), lax.rem(tau + DELAY, 2 * DELAY)
        sent = not static or stage_of(tau) < far

        def take():
            for way in (0, 1):
                message(tau - DELAY, way, lowest(tau - DELAY)).wait()

        def fresh():
            exchange(tau - 1).wait()

        if not static or stage_of(tau - DELAY) < far:
            when(tau >= 1 + DELAY, take)
        if not static or tau - 1 < tickets:
            when(tau >= 1, fresh)

        def work():
            for way in (0, 1):
                sign = 1 if way == 0 else -1
                for stage in range(stage_of(tau), far):
                    u, chip = tau - 1 - DELAY * stage, at(sign * (far - stage))
                    for part in (way, 1 - way) if stage else (way,):
                        total = own_term(u, chip, part)
                        if stage > 1 or (stage == 1 and part == way):
                            total += RECV[way, came, spot(stage - 1, way, part)].astype(F32)
                        SEND[way, box, spot(stage, way, part)] = total.astype(BF16)
            if sent:
                for way in (0, 1):
                    message(tau, way, lowest(tau)).start()

        def final():
            u = tau - 1 - DELAY * far
            total = [(RECV[0, came, spot(far - 1, 0, part)].astype(F32) + RECV[1, came, spot(far - 1, 1, part)].astype(F32)
                      + own_term(u, z, part)).astype(BF16) for part in (0, 1)]
            l, place = 1 - u // layer_slots, u % layer_slots

            def gate_up():
                cols = pl.ds(pl.multiple_of(place * fb, fb), fb)
                OG[l, :, cols] = total[0]
                OU[l, :, cols] = total[1]

            def down():
                rows = pl.ds(pl.multiple_of((place - blocks) * rb, rb), rb)
                for part in (0, 1):
                    OD[l, rows, pl.ds(part * fb, fb)] = total[part]

            when(place < blocks, gate_up)
            when(place >= blocks, down)

        when(tau >= 1 + DELAY * far, final)
        when(tau >= 1, work)

    def issue(tau):
        reduce_step(tau)
        when(tau >= 0, lambda: exchange(tau).start())

    def down_ticket(tau, k):
        for b in range(2 * n):
            TK[ticket_row(tau, b % 2), b // 2] = DWD[pl.ds(pl.multiple_of(b * db + k * rb, rb), rb), :]

    def gradients(j):
        tau_rows = pl.ds(pl.multiple_of(j * fb, fb), fb)
        before = lax.rem(j, blocks) if not isinstance(j, int) else j % blocks

        def part(m, tau):
            if m < 2:
                dw = dot(AT[...], DGU[:, columns(before)[m]]).astype(BF16)
                for b in range(2 * n):
                    TK[ticket_row(tau, b % 2), b // 2, :, pl.ds(m * fb, fb)] = dw[b * rb:(b + 1) * rb]
            else:
                DWD[tau_rows, :] = dot(DYT[...], PJ[...]).T.astype(BF16)

        return part

    def bw_layer(i, _):
        l = 1 - i
        base = i * layer_slots

        def block(j, _):
            tau = base + j - 1

            @pl.when((i == 0) & (j == 2))
            def _():
                ag_round(ready_round(5))

            @pl.when((i == 0) & (j == per_half))
            def _():
                partner_wait(5).wait_recv()

            gc, uc = columns(j)
            wg, wu = WGU[l, :, gc], WGU[l, :, uc]
            wd = WD[l, pl.ds(pl.multiple_of(j * fb, fb), fb), :]
            part = gradients(lax.rem(j + blocks, blocks + 1))
            part(2, tau)
            for q in range(tiles):
                ts = pl.ds(q * tile, tile)
                a = A[ts, :]
                dp = dot_t(DY[ts, :], wd).astype(BF16)
                g, u = dot(a, wg), dot(a, wu)
                if q < 2:
                    part(q, tau)
                dp = dp.astype(F32)
                s = 0.5 * jnp.tanh(0.5 * g) + 0.5
                gs = g * s
                PJ[ts, :] = (gs * u).astype(BF16)
                DGU[ts, uc] = (dp * gs).astype(BF16)
                DGU[ts, gc] = (dp * u * (s + gs * (1.0 - s))).astype(BF16)

            @pl.when(j == 0)
            def _():
                down_ticket(tau, kw - 1)

            issue(tau)
            return 0

        lax.fori_loop(0, blocks, block, 0)

        def tail_slot(k, _):
            tau = base + blocks - 1 + k

            @pl.when(k == 0)
            def _():
                part = gradients(blocks - 1)
                for m in range(3):
                    part(m, tau)

            @pl.when(k < tiles_c)
            def _():
                ts = pl.ds(pl.multiple_of(k * tile_c, tile_c), tile_c)
                da = dot_t(DGU[ts, :], WGU[l]).astype(BF16).astype(F32)
                wide = H[ts, :].astype(F32)
                scale = rms_scale(wide)
                dwide = da * scale - wide * (scale * scale * scale * jnp.mean(da * wide, -1, keepdims=True))
                DY[ts, :] = DY[ts, :] + dwide.astype(BF16)

            @pl.when((k == tiles_c) & (i == 0))
            def _():
                load_x.start()
                load_x.wait()
                normed_into(True)
                transpose_dy()

            @pl.when(k > 0)
            def _():
                down_ticket(tau, k - 1)

            issue(tau)
            return 0

        lax.fori_loop(0, kw, tail_slot, 0)
        return 0

    lax.fori_loop(0, 2, bw_layer, 0)

    out_x = pltpu.make_async_copy(DY, dx_hbm.at[0], out_sem.at[0])
    out_x.start()
    down_ticket(tickets - 1, kw - 1)
    for tau in range(tickets - 1, tickets + DELAY * far + 1):
        reduce_step(tau)
        if tau == tickets - 1:
            exchange(tau).start()
    outs = [pltpu.make_async_copy(a, b, out_sem.at[1 + m]) for m, (a, b) in enumerate(((OG, g_hbm), (OU, u_hbm), (OD, d_hbm)))]
    for copy in outs:
        copy.start()
    for t in range(len(AG)):
        for k in range(n // 2):
            for way in (0, 1):
                hop(t, k, way).wait_send()
        if xy:
            for m in (0, 1):
                group_wait(t, m).wait_send()
        partner_wait(t).wait_send()
    for copy in [out_x, *outs]:
        copy.wait()


def solution(mesh):
    groups = mesh.shape["rep"]
    n = mesh.shape["dp"] // 2
    side = math.isqrt(groups)
    xy = groups > 1

    def step(x, dy, w_gate, w_up, w_down):
        _, tokens, d = x.shape
        layers, _, ff = w_gate.shape
        rb = d // (2 * n)
        fb = d // 2
        ring = DELAY * (n // 2) + 2
        dma = pltpu.SemaphoreType.DMA
        call = pl.pallas_call(
            functools.partial(kernel, (n, side, xy, tokens, d, ff)),
            out_shape=(jax.ShapeDtypeStruct((1, tokens, d), BF16), jax.ShapeDtypeStruct((layers, rb, ff), BF16),
                       jax.ShapeDtypeStruct((layers, rb, ff), BF16), jax.ShapeDtypeStruct((layers, ff // (2 * n), d), BF16)),
            in_specs=[pl.BlockSpec(memory_space=pl.ANY)] * 5,
            out_specs=(pl.BlockSpec(memory_space=pl.ANY),) * 4,
            scratch_shapes=[
                pltpu.VMEM((layers, d, 2 * ff), BF16),
                pltpu.VMEM((layers, ff, d), BF16),
                pltpu.VMEM((tokens, d), BF16),
                pltpu.VMEM((tokens, d), BF16),
                pltpu.VMEM((d, tokens), BF16),
                pltpu.VMEM((tokens, d), BF16),
                pltpu.VMEM((d, tokens), BF16),
                pltpu.VMEM((tokens, 2 * ff), BF16),
                pltpu.VMEM((tokens, fb), BF16),
                pltpu.VMEM((ff + fb, d), BF16),
                pltpu.VMEM((ring + 2, n, rb, d), BF16),
                pltpu.VMEM((ring, n, rb, d), BF16),
                pltpu.VMEM((2, 2 * DELAY, n - 1, rb, fb), BF16),
                pltpu.VMEM((2, 2 * DELAY, n - 1, rb, fb), BF16),
                pltpu.VMEM((layers, rb, ff), BF16),
                pltpu.VMEM((layers, rb, ff), BF16),
                pltpu.VMEM((layers, ff // (2 * n), d), BF16),
                dma((14,)), dma((6, n // 2, 2)), dma((6, n // 2, 2)), dma((6, 2)), dma((6, 2)), dma((6,)), dma((6,)),
                dma((2,)), dma((2,)), dma((2, 2 * DELAY)), dma((2, 2 * DELAY)), dma((4,)),
            ],
            compiler_params=pltpu.CompilerParams(collective_id=0, has_side_effects=True, vmem_limit_bytes=67043328),
        )

        seqs, rows = P(("rep", "dp")), P(None, "dp")
        return jax.shard_map(call, mesh=mesh, in_specs=(seqs, seqs, rows, rows, rows),
                             out_specs=(seqs, P("rep", "dp"), P("rep", "dp"), P("rep", "dp")), check_vma=False)(x, dy, w_gate, w_up, w_down)

    return step
```

time: 911 us -> 210 us (0.23); the launches traced: 900 us -> 210 us
  matrix products: 311 us -> 0 us
  waiting for transfers between devices: 215 us -> 0 us
  Pallas kernels: 0 us -> 204 us
  starting transfers between devices: 145 us -> 0 us
  other arithmetic: 98.5 us -> 0 us
  local copies, waits for them, and re-layouts: 68.4 us -> 5.31 us
  loops' own time: 46.7 us -> 0 us
  between operations: 15.1 us -> 0.67 us
    dot_general x59 -> x0, matrix products: 311 us -> none  [the longest x20 120 us: layer(): gate = jnp.dot(a, w['w_gate'], preferred_element_type=jnp.float32)]
    pallas_call x0 -> x1, Pallas kernels: none -> 204 us  [step(): jax.shard_map(call, mesh=mesh, in_specs=(seqs, seqs, rows, rows, rows), o...]
    dot_general x102 -> x0, starting transfers between devices: 145 us -> none  [the longest x34 48.6 us: layer(): up = jnp.dot(a, w['w_up'], preferred_element_type=jnp.float32)]
    squeeze x6 -> x0, waiting for transfers between devices: 130 us -> none  [stack(): h = layer(h, {name: w[number] for name, w in weights.items()})]
    dot_general x102 -> x0, waiting for transfers between devices: 82.6 us -> none  [the longest x34 31.3 us: matmul(): jnp.dot(a, w, preferred_element_type=jnp.float32).astype(jnp.bfloat16)]
    dot_general x96 -> x0, other arithmetic: 64.1 us -> none
    another operation x6 -> x0, loops' own time: 46.7 us -> none  [the longest x2 16.2 us: layer(): up = jnp.dot(a, w['w_up'], preferred_element_type=jnp.float32)]
    unnamed x77 -> x10, local copies, waits for them, and re-layouts: 48.1 us -> 5.31 us
  transfers between devices with their start and end apart: 108 -> 0, of which waited for: 32 -> 0; matrix products, arithmetic and copies ran while one was open for 45% -> 0% of each run, Pallas kernels for 0% -> 0%
where the time goes in v1:
time: 210 us
  Pallas kernels  204 us (97%)
  local copies, waits for them, and re-layouts  5.31 us (3%)
    pallas_call x1, Pallas kernels, step(): jax.shard_map(call, mesh=mesh, in_specs=(seqs, seqs, rows, rows, rows), o...  204 us
    unnamed x10, local copies, waits for them, and re-layouts  5.31 us

profile of v1, /device:TPU:22, one launch (start us, length us, event | category | flops | bytes accessed | tf_op | source)
XLA Modules:
  0.0 210.3 jit_solution(15844381691808577183)
XLA Ops:
  0.6 204.3 %shard_map.84 = (bf16[1,2048,512]{2,1,0:T(8,128)(2,1)}, bf16[2,32,2560]{2,1,0:T(8,128)(2,1)}, bf16[2,32,2560]{2,1,0:T(8,128)(2,1)}, bf16[2,160,512]{2,1,0:T(8,128)(2,1)}) custom-call(bf16[1,2048,512]{2,1,0:T(8,128)(2,1)} %x_hbm.1, bf16[1,2048,512]{2,1,0:T(8,128)(2,1)} %dy_hbm.1, bf16[2,32,2560]{2,1,0:T(8,128)(2,1)} %wg_hbm.1, bf16[2,32,2560]{2,1,0:T(8,128)(2,1)} %wu_hbm.1, ...), custom_call_target="tpu_custom_call" | custom-call | tf_op jit(solution)/shard_map/pallas_call | solution.py:494
  204.9 0.0 copy-start.2
  204.9 0.0 copy-start.1
  204.9 0.0 copy-start
  204.9 3.1 %copy.13 = bf16[1,2048,512]{2,1,0:T(8,128)(2,1)} copy(bf16[1,2048,512]{2,1,0:T(8,128)(2,1)} %get-tuple-element.8) | data formatting | bytes 4194304
  208.1 0.0 copy-done.2
  208.1 0.7 copy.14
  208.8 0.0 copy-done.1
  208.8 0.7 copy.15
  209.5 0.0 copy-done
  209.5 0.7 copy.16
Async XLA Ops:
  204.9 3.2 %copy-start.2 = (bf16[2,32,2560]{2,1,0:T(8,128)(2,1)S(1)}, bf16[2,32,2560]{2,1,0:T(8,128)(2,1)}, u32[]{:S(2)}) copy-start(bf16[2,32,2560]{2,1,0:T(8,128)(2,1)} %get-tuple-element.9) | copy-start | bytes 983044
  204.9 3.9 %copy-start.1 = (bf16[2,32,2560]{2,1,0:T(8,128)(2,1)S(1)}, bf16[2,32,2560]{2,1,0:T(8,128)(2,1)}, u32[]{:S(2)}) copy-start(bf16[2,32,2560]{2,1,0:T(8,128)(2,1)} %get-tuple-element.10) | copy-start | bytes 983044
  204.9 4.6 %copy-start = (bf16[2,160,512]{2,1,0:T(8,128)(2,1)S(1)}, bf16[2,160,512]{2,1,0:T(8,128)(2,1)}, u32[]{:S(2)}) copy-start(bf16[2,160,512]{2,1,0:T(8,128)(2,1)} %get-tuple-element.11) | copy-start | bytes 983044

commit v2 on v1

--- a/solution.py
+++ b/solution.py
@@ -162,8 +162,12 @@
 
     def ag_round(r):
         for t in range(len(AG)):
-            if 0 <= r - t <= last:
+            if t == 0 and r == 0:
+                ag_step(0, 0)
+            elif 1 <= r - t <= last:
                 ag_step(t, r - t)
+            elif t == r + 1:
+                ag_step(t, 0)
 
     def ready_round(t):
         return t + last
@@ -237,7 +241,7 @@
         return lax.rem(u + 4 * ring, ring)
 
     def exchange(u):
-        par = lax.rem(u, 2)
+        par = lax.rem(u + 2, 2)
         return remote(TK.at[ring + par], SIB.at[slot_of(u)], tk_send.at[par], tk_recv.at[par], partner)
 
     def message(tau, way, lo):
@@ -270,10 +274,12 @@
     def spot(stage, way, part):
         return 0 if stage == 0 else 2 * stage - 1 + (part != way)
 
-    def reduce_step(tau):
+    def came_in(tau):
+        return lax.rem(tau + DELAY, 2 * DELAY)
+
+    def collect(tau):
         static = isinstance(tau, int)
-        box, came = lax.rem(tau + 2 * DELAY, 2 * DELAY), lax.rem(tau + DELAY, 2 * DELAY)
-        sent = not static or stage_of(tau) < far
+        came = came_in(tau)
 
         def take():
             for way in (0, 1):
@@ -281,25 +287,6 @@
 
         def fresh():
             exchange(tau - 1).wait()
-
-        if not static or stage_of(tau - DELAY) < far:
-            when(tau >= 1 + DELAY, take)
-        if not static or tau - 1 < tickets:
-            when(tau >= 1, fresh)
-
-        def work():
-            for way in (0, 1):
-                sign = 1 if way == 0 else -1
-                for stage in range(stage_of(tau), far):
-                    u, chip = tau - 1 - DELAY * stage, at(sign * (far - stage))
-                    for part in (way, 1 - way) if stage else (way,):
-                        total = own_term(u, chip, part)
-                        if stage > 1 or (stage == 1 and part == way):
-                            total += RECV[way, came, spot(stage - 1, way, part)].astype(F32)
-                        SEND[way, box, spot(stage, way, part)] = total.astype(BF16)
-            if sent:
-                for way in (0, 1):
-                    message(tau, way, lowest(tau)).start()
 
         def final():
             u = tau - 1 - DELAY * far
@@ -320,12 +307,32 @@
             when(place < blocks, gate_up)
             when(place >= blocks, down)
 
+        if not static or stage_of(tau - DELAY) < far:
+            when(tau >= DELAY - 1, take)
+        if not static or tau - 1 < tickets:
+            when(tau >= 0, fresh)
         when(tau >= 1 + DELAY * far, final)
-        when(tau >= 1, work)
+
+    def combine(tau):
+        box = lax.rem(tau + 2 * DELAY, 2 * DELAY)
+        for way in (0, 1):
+            sign = 1 if way == 0 else -1
+            for stage in range(stage_of(tau), far):
+                u, chip = tau - 1 - DELAY * stage, at(sign * (far - stage))
+                for part in (way, 1 - way) if stage else (way,):
+                    total = own_term(u, chip, part)
+                    if stage > 1 or (stage == 1 and part == way):
+                        total += RECV[way, came_in(tau), spot(stage - 1, way, part)].astype(F32)
+                    SEND[way, box, spot(stage, way, part)] = total.astype(BF16)
+
+    def send(tau):
+        if stage_of(tau) < far:
+            for way in (0, 1):
+                message(tau, way, lowest(tau)).start()
 
     def issue(tau):
-        reduce_step(tau)
-        when(tau >= 0, lambda: exchange(tau).start())
+        send(tau)
+        exchange(tau).start()
 
     def down_ticket(tau, k):
         for b in range(2 * n):
@@ -370,8 +377,8 @@
                 a = A[ts, :]
                 dp = dot_t(DY[ts, :], wd).astype(BF16)
                 g, u = dot(a, wg), dot(a, wu)
-                if q < 2:
-                    part(q, tau)
+                if q % 2 == 0:
+                    part(q // 2, tau)
                 dp = dp.astype(F32)
                 s = 0.5 * jnp.tanh(0.5 * g) + 0.5
                 gs = g * s
@@ -383,6 +390,8 @@
             def _():
                 down_ticket(tau, kw - 1)
 
+            collect(tau)
+            combine(tau)
             issue(tau)
             return 0
 
@@ -417,6 +426,8 @@
             def _():
                 down_ticket(tau, k - 1)
 
+            collect(tau)
+            combine(tau)
             issue(tau)
             return 0
 
@@ -429,7 +440,9 @@
     out_x.start()
     down_ticket(tickets - 1, kw - 1)
     for tau in range(tickets - 1, tickets + DELAY * far + 1):
-        reduce_step(tau)
+        collect(tau)
+        combine(tau)
+        send(tau)
         if tau == tickets - 1:
             exchange(tau).start()
     outs = [pltpu.make_async_copy(a, b, out_sem.at[1 + m]) for m, (a, b) in enumerate(((OG, g_hbm), (OU, u_hbm), (OD, d_hbm)))]

time: 210 us -> 207 us (0.986)
  Pallas kernels: 204 us -> 201 us
    pallas_call x1, Pallas kernels: 204 us -> 201 us  [step(): jax.shard_map(call, mesh=mesh, in_specs=(seqs, seqs, rows, rows, rows), o...]
where the time goes in v2:
time: 207 us
  Pallas kernels  201 us (97%)
  local copies, waits for them, and re-layouts  5.31 us (3%)
    pallas_call x1, Pallas kernels, step(): jax.shard_map(call, mesh=mesh, in_specs=(seqs, seqs, rows, rows, rows), o...  201 us
    unnamed x10, local copies, waits for them, and re-layouts  5.31 us

profile of v2, /device:TPU:22, one launch (start us, length us, event | category | flops | bytes accessed | tf_op | source)
XLA Modules:
  0.0 206.9 jit_solution(3313380499015309186)
XLA Ops:
  0.6 201.0 %shard_map.84 = (bf16[1,2048,512]{2,1,0:T(8,128)(2,1)}, bf16[2,32,2560]{2,1,0:T(8,128)(2,1)}, bf16[2,32,2560]{2,1,0:T(8,128)(2,1)}, bf16[2,160,512]{2,1,0:T(8,128)(2,1)}) custom-call(bf16[1,2048,512]{2,1,0:T(8,128)(2,1)} %x_hbm.1, bf16[1,2048,512]{2,1,0:T(8,128)(2,1)} %dy_hbm.1, bf16[2,32,2560]{2,1,0:T(8,128)(2,1)} %wg_hbm.1, bf16[2,32,2560]{2,1,0:T(8,128)(2,1)} %wu_hbm.1, ...), custom_call_target="tpu_custom_call" | custom-call | tf_op jit(solution)/shard_map/pallas_call | solution.py:507
  201.6 0.0 copy-start.2
  201.6 0.0 copy-start.1
  201.6 0.0 copy-start
  201.6 3.1 %copy.13 = bf16[1,2048,512]{2,1,0:T(8,128)(2,1)} copy(bf16[1,2048,512]{2,1,0:T(8,128)(2,1)} %get-tuple-element.8) | data formatting | bytes 4194304
  204.8 0.0 copy-done.2
  204.8 0.7 copy.14
  205.5 0.0 copy-done.1
  205.5 0.7 copy.15
  206.2 0.0 copy-done
  206.2 0.7 copy.16
Async XLA Ops:
  201.6 3.2 %copy-start.2 = (bf16[2,32,2560]{2,1,0:T(8,128)(2,1)S(1)}, bf16[2,32,2560]{2,1,0:T(8,128)(2,1)}, u32[]{:S(2)}) copy-start(bf16[2,32,2560]{2,1,0:T(8,128)(2,1)} %get-tuple-element.9) | copy-start | bytes 983044
  201.6 3.9 %copy-start.1 = (bf16[2,32,2560]{2,1,0:T(8,128)(2,1)S(1)}, bf16[2,32,2560]{2,1,0:T(8,128)(2,1)}, u32[]{:S(2)}) copy-start(bf16[2,32,2560]{2,1,0:T(8,128)(2,1)} %get-tuple-element.10) | copy-start | bytes 983044
  201.6 4.6 %copy-start = (bf16[2,160,512]{2,1,0:T(8,128)(2,1)S(1)}, bf16[2,160,512]{2,1,0:T(8,128)(2,1)}, u32[]{:S(2)}) copy-start(bf16[2,160,512]{2,1,0:T(8,128)(2,1)} %get-tuple-element.11) | copy-start | bytes 983044
